TPU v7x, 32 devices: a whole 2x2x4 slice. The times are simulated.
32 devices in a mesh: prow: 8 (over z, y), pcol: 4 (over x, core).
Axes of the slice: x: 2, y: 2, z: 4, core: 2. Of those that a mesh axis runs over, the one named last changes fastest.
Arguments:
- inverse_block: bfloat16 [2, 512, 512], P(None, 'prow', 'pcol'), may hold values from -1.75 to 1.75
- panel: bfloat16 [2, 512, 2048], P(None, ('prow', 'pcol')), may hold values from -0.5 to 0.5
- pattern: int32 [1, 4], replicated, may hold values 0 or 1
- diag_inverse: float32 [2, 512, 2048], P(None, None, 'pcol'), may hold values from -6 to 6
Outputs:
- offdiag: bfloat16 [2, 512, 2048], P(None, 'prow', 'pcol')
- diagonal: float32 [2, 512, 2048], P(None, None, 'pcol')
All inputs are finite; a program needn't handle non-finite values.
Results may differ from a plain program's by a relative error of at most 0.0024.
Values may be sent and summed in bfloat16 or wider, within the bound.
A program may use at most 64 MiB of HBM per device.

v0:
```python
import jax
import jax.numpy as jnp
from jax import lax
from jax.sharding import PartitionSpec as P

WIDTH = 512


def complex_product(left_real, left_imag, right_real, right_imag, contract):
    dims = (((contract,), (0,)), ((), ()))
    real_part = lax.dot_general(
        left_real, right_real, dims, preferred_element_type=jnp.float32
    ) - lax.dot_general(left_imag, right_imag, dims, preferred_element_type=jnp.float32)
    imag_part = lax.dot_general(
        left_real, right_imag, dims, preferred_element_type=jnp.float32
    ) + lax.dot_general(left_imag, right_real, dims, preferred_element_type=jnp.float32)
    return (real_part, imag_part)


def keep_table(pattern, row_start, row_count, col_start, col_count, block_width):
    row_ids = (row_start + jnp.arange(row_count, dtype=jnp.int32)) // block_width
    col_ids = (col_start + jnp.arange(col_count, dtype=jnp.int32)) // block_width
    row_select = (
        row_ids[:, None] == jnp.arange(pattern.shape[0], dtype=jnp.int32)[None, :]
    ).astype(jnp.float32)
    col_select = (
        col_ids[:, None] == jnp.arange(pattern.shape[1], dtype=jnp.int32)[None, :]
    ).astype(jnp.float32)
    pattern_value = pattern.astype(jnp.float32)
    row_pattern = jnp.dot(row_select, pattern_value, precision=lax.Precision.HIGHEST)
    return jnp.dot(row_pattern, col_select.T, precision=lax.Precision.HIGHEST)


def local(inverse_block, panel, pattern, diag_inverse):
    rows_dev = inverse_block.shape[1]
    block_span = inverse_block.shape[2]
    fine_rows = panel.shape[1]
    columns = panel.shape[2]
    row_index = lax.axis_index("prow")
    col_index = lax.axis_index("pcol")
    col_count = lax.axis_size("pcol")
    root_count = lax.axis_size("prow") // col_count
    fine_start = (row_index * col_count + col_index) * fine_rows
    keep_mask = keep_table(pattern, fine_start, fine_rows, 0, columns, WIDTH)
    masked = jnp.where(keep_mask[None] > 0.5, panel, jnp.zeros_like(panel))
    row_panel = lax.all_gather(masked, "pcol", axis=1, tiled=True)
    flipped = jnp.swapaxes(inverse_block, 1, 2)
    split_cols = flipped.reshape(2, root_count, col_count, fine_rows, rows_dev)
    received = lax.all_to_all(split_cols, "pcol", split_axis=2, concat_axis=1, tiled=True)
    regrouped = received.reshape(2, block_span, rows_dev)
    panel_piece = lax.all_gather(masked, "prow", axis=1, tiled=True)
    part_real, part_imag = complex_product(
        regrouped[0], regrouped[1], panel_piece[0], panel_piece[1], 0
    )
    stacked = jnp.stack([part_real, part_imag])
    summed = lax.psum_scatter(stacked, "pcol", scatter_dimension=2, tiled=True)
    local_cols = summed.shape[2]
    keep_local = keep_table(
        pattern, row_index * rows_dev, rows_dev, col_index * local_cols, local_cols, WIDTH
    )
    coupled = (summed * keep_local[None]).astype(jnp.bfloat16)
    offdiag = -coupled
    block_start = col_index * local_cols // WIDTH * WIDTH
    lower_panel = lax.dynamic_slice_in_dim(row_panel, block_start, WIDTH, 2)
    diag_real, diag_imag = complex_product(
        lower_panel[0], lower_panel[1], coupled[0], coupled[1], 0
    )
    shares = lax.psum_scatter(
        jnp.stack([diag_real, diag_imag]), "prow", scatter_dimension=1, tiled=True
    )
    correction = lax.all_gather(shares, "prow", axis=1, tiled=True)
    return (offdiag, diag_inverse + correction)


def solution(mesh):
    in_specs = (
        P(None, "prow", "pcol"),
        P(None, ("prow", "pcol"), None),
        P(),
        P(None, None, "pcol"),
    )
    out_specs = (P(None, "prow", "pcol"), P(None, None, "pcol"))
    return jax.shard_map(local, mesh=mesh, in_specs=in_specs, out_specs=out_specs, check_vma=False)
```

profile of v0, /device:TPU:0, one launch (start us, length us, event | category | flops | bytes accessed | tf_op | source)
XLA Modules:
  0.0 214.8 jit_solution(16898340930722284187)
XLA Ops:
  7.2 0.7 convert_bitcast_fusion
  7.9 0.7 convolution_compare_fusion
  8.6 1.6 broadcast_select_fusion
  10.3 0.9 copy.9
  11.2 0.1 reshape.60
  11.3 8.0 %all_to_all.15 = bf16[4,2,2048]{2,1,0:T(2,128)(2,1)S(1)} all-to-all(bf16[4,2,2048]{2,1,0:T(2,128)(2,1)S(1)} %reshape.60), channel_id=1, replica_groups=mesh['prow'=8,'pcol'=4] {'pcol'}, dimensions={0} | all-to-all | bytes 65536 | tf_op jit(solution)/shard_map/all_to_all | solution.py:49
  19.4 34.3 %all-gather.3.cloned.1.call-done = bf16[2,128,2048]{2,1,0:T(8,128)(2,1)} async-done(((bf16[2,16,2048]{2,1,0:T(8,128)(2,1)}), bf16[2,128,2048]{2,1,0:T(8,128)(2,1)}) %all-gather.3.cloned.1.call-update) | async-done | bytes 1048592 | tf_op jit(solution)/shard_map/all_gather | solution.py:51
  53.7 1.4 fusion.6
  55.1 1.3 fusion.5
  56.5 0.3 fusion.1
  56.8 0.3 fusion
  57.0 1.0 pad_maximum_fusion.1
  58.2 7.2 %all_gather.10 = bf16[2,64,2048]{2,1,0:T(8,128)(2,1)S(1)} all-gather(bf16[2,16,2048]{2,1,0:T(8,128)(2,1)S(1)} %copy-done.2), channel_id=1, replica_groups=mesh['prow'=8,'pcol'=4] {'pcol'}, dimensions={1}, use_global_device_ids=true | all-gather | bytes 655360 | tf_op jit(solution)/shard_map/all_gather | solution.py:46
  65.4 0.4 fusion.7
  65.7 16.0 %reduce-scatter.3.cloned.1.call-done = f32[2,64,512]{2,1,0:T(8,128)} async-done(((f32[2,64,2048]{2,1,0:T(8,128)}), f32[2,64,512]{2,1,0:T(8,128)}) %reduce-scatter.3.cloned.1.call-update) | async-done | bytes 262160 | tf_op jit(solution)/shard_map/reduce_scatter | solution.py:56
  81.8 1.6 fusion.27
  83.4 0.3 fusion.9
  83.8 0.3 fusion.10
  84.1 0.3 fusion.3
  84.4 0.3 fusion.2
  84.7 1.5 pad_maximum_fusion
  86.3 68.4 %reduce-scatter.5.cloned.1.call-done = f32[2,64,512]{2,1,0:T(8,128)} async-done(((f32[2,512,512]{2,1,0:T(8,128)}), f32[2,64,512]{2,1,0:T(8,128)}) %reduce-scatter.5.cloned.1.call-update) | async-done | bytes 262160 | tf_op jit(solution)/shard_map/reduce_scatter | solution.py:68
  154.8 50.1 %all-gather.5.cloned.1.call-done = f32[2,512,512]{2,1,0:T(8,128)} async-done(((f32[2,64,512]{2,1,0:T(8,128)}), f32[2,512,512]{2,1,0:T(8,128)}) %all-gather.5.cloned.1.call-update) | async-done | bytes 2097168 | tf_op jit(solution)/shard_map/all_gather | solution.py:71
  204.9 3.4 %add.76 = f32[2,512,512]{2,1,0:T(8,128)} add(f32[2,512,512]{2,1,0:T(8,128)S(1)} %copy-done.1, f32[2,512,512]{2,1,0:T(8,128)} %all-gather.5.cloned.1.call-done) | non-fusion elementwise | flops 524288 | bytes 6291456 | tf_op jit(solution)/shard_map/add | solution.py:72
  (22 shorter events, 0.4 us)
Async XLA Ops:
  7.2 46.6 %all-gather.3.cloned.1.call-start = ((), (), s32[]{:S(2)}) async-start(), calls=%async_computation.3 | async-start | bytes 1179648 | tf_op jit(solution)/shard_map/all_gather | solution.py:51
  10.2 71.5 %reduce-scatter.3.cloned.1.call-start = ((), (), s32[]{:S(2)}) async-start(), calls=%async_computation.4 | async-start | bytes 1310720 | tf_op jit(solution)/shard_map/reduce_scatter | solution.py:56
  53.7 2.7 %copy-start = (bf16[2,128,2048]{2,1,0:T(8,128)(2,1)S(1)}, bf16[2,128,2048]{2,1,0:T(8,128)(2,1)}, u32[]{:S(2)}) copy-start(bf16[2,128,2048]{2,1,0:T(8,128)(2,1)} %all-gather.3.cloned.1.call-done) | copy-start | bytes 3145732
  56.7 1.5 copy-start.2
  58.1 96.6 %reduce-scatter.5.cloned.1.call-start = ((), (), s32[]{:S(2)}) async-start(), calls=%async_computation.5 | async-start | bytes 2359296 | tf_op jit(solution)/shard_map/reduce_scatter | solution.py:68
  86.2 118.6 %copy-start.1 = (f32[2,512,512]{2,1,0:T(8,128)S(1)}, f32[2,512,512]{2,1,0:T(8,128)}, u32[]{:S(2)}) copy-start(f32[2,512,512]{2,1,0:T(8,128)} %param.7) | copy-start | bytes 6291460
  86.3 118.6 %all-gather.5.cloned.1.call-start = ((), (), s32[]{:S(2)}) async-start(), calls=%async_computation.6 | async-start | bytes 2359296 | tf_op jit(solution)/shard_map/all_gather | solution.py:71
Sparse Core Ops, SparseCore 0:
  10.7 42.9 all-gather.2
  58.2 23.5 reduce-scatter.2
  86.4 68.3 reduce-scatter.4
  156.8 48.0 all-gather.4
where the time goes:
time: 215 us
  waiting for transfers between devices  169 us (79%)
  blocking collectives  15.1 us (7%)
  between operations  13.9 us (6%)
  other arithmetic  9.83 us (5%)
  matrix products  5.66 us (3%)
    reduce_scatter x1, waiting for transfers between devices, local(): lax.psum_scatter(jnp.stack([diag_real, diag_imag]), 'prow', scatter_dimen...  68.4 us
    all_gather x1, waiting for transfers between devices, local(): correction = lax.all_gather(shares, 'prow', axis=1, tiled=True)  50.1 us
    all_gather x1, waiting for transfers between devices, local(): panel_piece = lax.all_gather(masked, 'prow', axis=1, tiled=True)  34.3 us
    reduce_scatter x1, waiting for transfers between devices, local(): summed = lax.psum_scatter(stacked, 'pcol', scatter_dimension=2, tiled=True)  16 us
    all_to_all x1, blocking collectives, local(): lax.all_to_all(split_cols, 'pcol', split_axis=2, concat_axis=1, tiled=True)  7.98 us
    all_gather x1, blocking collectives, local(): row_panel = lax.all_gather(masked, 'pcol', axis=1, tiled=True)  7.15 us
  transfers between devices with their start and end apart: 4, of which 4 were waited for; matrix products, arithmetic and copies ran while one was open for 1% of the time, Pallas kernels for 0%

commit v1 on v0

--- a/solution.py
+++ b/solution.py
@@ -48,7 +48,12 @@
     split_cols = flipped.reshape(2, root_count, col_count, fine_rows, rows_dev)
     received = lax.all_to_all(split_cols, "pcol", split_axis=2, concat_axis=1, tiled=True)
     regrouped = received.reshape(2, block_span, rows_dev)
-    panel_piece = lax.all_gather(masked, "prow", axis=1, tiled=True)
+    ring = [masked]
+    for hop in range(7):
+        ring.append(lax.ppermute(ring[-1], "prow", [(dev, (dev + 1) % 8) for dev in range(8)]))
+    panel_piece = jnp.roll(
+        jnp.concatenate(ring[::-1], axis=1), (lax.axis_index("prow") + 1) * ring[0].shape[1], axis=1
+    )
     part_real, part_imag = complex_product(
         regrouped[0], regrouped[1], panel_piece[0], panel_piece[1], 0
     )

time: 215 us -> 224 us (1.042)
  waiting for transfers between devices: 169 us -> 182 us
  blocking collectives: 15.1 us -> 6.5 us
  starting transfers between devices: 0.16 us -> 6.51 us
    ppermute x0 -> x7, waiting for transfers between devices: none -> 45.3 us  [local(): lax.ppermute(ring[-1], 'prow', [(dev, (dev + 1) % 8) for dev in range(8)])]
    all_gather x1 -> x0, waiting for transfers between devices: 34.3 us -> none  [local(): panel_piece = lax.all_gather(masked, 'prow', axis=1, tiled=True)]
    all_to_all x1 -> x0, blocking collectives: 7.98 us -> none  [local(): lax.all_to_all(split_cols, 'pcol', split_axis=2, concat_axis=1, tiled=True)]
    all_to_all x0 -> x1, waiting for transfers between devices: none -> 3.84 us  [local(): lax.all_to_all(split_cols, 'pcol', split_axis=2, concat_axis=1, tiled=True)]
    all_to_all x0 -> x1, starting transfers between devices: none -> 3.26 us  [local(): lax.all_to_all(split_cols, 'pcol', split_axis=2, concat_axis=1, tiled=True)]
    ppermute x0 -> x7, starting transfers between devices: none -> 3.12 us  [local(): lax.ppermute(ring[-1], 'prow', [(dev, (dev + 1) % 8) for dev in range(8)])]
  transfers between devices with their start and end apart: 4 -> 11, of which waited for: 4 -> 10; matrix products, arithmetic and copies ran while one was open for 1% -> 1% of each run, Pallas kernels for 0% -> 0%
where the time goes in v1:
time: 224 us
  waiting for transfers between devices  182 us (81%)
  between operations  14.1 us (6%)
  other arithmetic  9.27 us (4%)
  starting transfers between devices  6.51 us (3%)
  blocking collectives  6.5 us (3%)
  matrix products  3.51 us (2%)
    reduce_scatter x1, waiting for transfers between devices, local(): lax.psum_scatter(jnp.stack([diag_real, diag_imag]), 'prow', scatter_dimen...  68.7 us
    all_gather x1, waiting for transfers between devices, local(): correction = lax.all_gather(shares, 'prow', axis=1, tiled=True)  50.3 us
    ppermute x7, waiting for transfers between devices, local(): lax.ppermute(ring[-1], 'prow', [(dev, (dev + 1) % 8) for dev in range(8)])  45.3 us
    reduce_scatter x1, waiting for transfers between devices, local(): summed = lax.psum_scatter(stacked, 'pcol', scatter_dimension=2, tiled=True)  13.8 us
    all_gather x1, blocking collectives, local(): row_panel = lax.all_gather(masked, 'pcol', axis=1, tiled=True)  6.5 us
  transfers between devices with their start and end apart: 11, of which 10 were waited for; matrix products, arithmetic and copies ran while one was open for 1% of the time, Pallas kernels for 0%

profile of v1, /device:TPU:0, one launch (start us, length us, event | category | flops | bytes accessed | tf_op | source)
XLA Modules:
  0.0 223.7 jit_solution(4579817308020850942)
XLA Ops:
  7.2 0.7 convert_bitcast_fusion
  7.9 0.7 convolution_compare_fusion
  8.6 0.9 broadcast_select_fusion
  9.6 3.0 %collective-permute-start = (bf16[2,16,2048]{2,1,0:T(8,128)(2,1)S(1)}, bf16[2,16,2048]{2,1,0:T(8,128)(2,1)S(1)}, u32[]{:S(2)}, u32[]{:S(2)}) collective-permute-start(bf16[2,16,2048]{2,1,0:T(8,128)(2,1)S(1)} %broadcast_select_fusion), channel_id=1, source_target_pairs={{0,4},{4,8},{8,12},{12,16},{16,20},{20,24},{24,28},{28,0},{1,5},{5... | collective-permute-start | bytes 393224 | tf_op jit(solution)/shard_map/ppermute | solution.py:53
  12.6 6.5 %collective-permute-done = bf16[2,16,2048]{2,1,0:T(8,128)(2,1)S(1)} collective-permute-done((bf16[2,16,2048]{2,1,0:T(8,128)(2,1)S(1)}, bf16[2,16,2048]{2,1,0:T(8,128)(2,1)S(1)}, u32[]{:S(2)}, u32[]{:S(2)}) %collective-permute-start) | collective-permute-done | bytes 131104 | tf_op jit(solution)/shard_map/ppermute | solution.py:53
  19.2 7.7 %collective-permute-done.1 = bf16[2,16,2048]{2,1,0:T(8,128)(2,1)S(1)} collective-permute-done((bf16[2,16,2048]{2,1,0:T(8,128)(2,1)S(1)}, bf16[2,16,2048]{2,1,0:T(8,128)(2,1)S(1)}, u32[]{:S(2)}, u32[]{:S(2)}) %collective-permute-start.1) | collective-permute-done | bytes 131104 | tf_op jit(solution)/shard_map/ppermute | solution.py:53
  26.8 7.7 %collective-permute-done.2 = bf16[2,16,2048]{2,1,0:T(8,128)(2,1)S(1)} collective-permute-done((bf16[2,16,2048]{2,1,0:T(8,128)(2,1)S(1)}, bf16[2,16,2048]{2,1,0:T(8,128)(2,1)S(1)}, u32[]{:S(2)}, u32[]{:S(2)}) %collective-permute-start.2) | collective-permute-done | bytes 131104 | tf_op jit(solution)/shard_map/ppermute | solution.py:53
  34.5 7.7 %collective-permute-done.3 = bf16[2,16,2048]{2,1,0:T(8,128)(2,1)S(1)} collective-permute-done((bf16[2,16,2048]{2,1,0:T(8,128)(2,1)S(1)}, bf16[2,16,2048]{2,1,0:T(8,128)(2,1)S(1)}, u32[]{:S(2)}, u32[]{:S(2)}) %collective-permute-start.3) | collective-permute-done | bytes 131104 | tf_op jit(solution)/shard_map/ppermute | solution.py:53
  42.2 0.9 copy.9
  43.0 0.7 reshape.60
  43.8 3.3 %all-to-all-start = ((bf16[4,2,2048]{2,1,0:T(2,128)(2,1)}), bf16[4,2,2048]{2,1,0:T(2,128)(2,1)S(1)}, u32[]{:S(2)}, u32[]{:S(2)}) async-start(bf16[4,2,2048]{2,1,0:T(2,128)(2,1)} %reshape.60), calls=%async_computation | async-start | bytes 65536 | tf_op jit(solution)/shard_map/all_to_all | solution.py:49
  47.1 3.8 %all-to-all-done = bf16[4,2,2048]{2,1,0:T(2,128)(2,1)S(1)} async-done(((bf16[4,2,2048]{2,1,0:T(2,128)(2,1)}), bf16[4,2,2048]{2,1,0:T(2,128)(2,1)S(1)}, u32[]{:S(2)}, u32[]{:S(2)}) %all-to-all-start) | async-done | bytes 32800 | tf_op jit(solution)/shard_map/all_to_all | solution.py:49
  51.2 8.1 %collective-permute-done.5 = bf16[2,16,2048]{2,1,0:T(8,128)(2,1)S(1)} collective-permute-done((bf16[2,16,2048]{2,1,0:T(8,128)(2,1)S(1)}, bf16[2,16,2048]{2,1,0:T(8,128)(2,1)S(1)}, u32[]{:S(2)}, u32[]{:S(2)}) %collective-permute-start.5) | collective-permute-done | bytes 131104 | tf_op jit(solution)/shard_map/ppermute | solution.py:53
  59.3 7.7 %collective-permute-done.6 = bf16[2,16,2048]{2,1,0:T(8,128)(2,1)S(1)} collective-permute-done((bf16[2,16,2048]{2,1,0:T(8,128)(2,1)S(1)}, bf16[2,16,2048]{2,1,0:T(8,128)(2,1)S(1)}, u32[]{:S(2)}, u32[]{:S(2)}) %collective-permute-start.6) | collective-permute-done | bytes 131104 | tf_op jit(solution)/shard_map/ppermute | solution.py:53
  68.4 1.0 pad_maximum_fusion.1
  69.6 6.5 %all_gather.6 = bf16[2,64,2048]{2,1,0:T(8,128)(2,1)S(1)} all-gather(bf16[2,16,2048]{2,1,0:T(8,128)(2,1)S(1)} %broadcast_select_fusion), channel_id=1, replica_groups=mesh['prow'=8,'pcol'=4] {'pcol'}, dimensions={1}, use_global_device_ids=true | all-gather | bytes 655360 | tf_op jit(solution)/shard_map/all_gather | solution.py:46
  76.1 0.4 fusion.7
  76.4 13.8 %reduce-scatter.3.cloned.1.call-done = f32[2,64,512]{2,1,0:T(8,128)} async-done(((f32[2,64,2048]{2,1,0:T(8,128)}), f32[2,64,512]{2,1,0:T(8,128)}) %reduce-scatter.3.cloned.1.call-update) | async-done | bytes 262160 | tf_op jit(solution)/shard_map/reduce_scatter | solution.py:61
  90.2 1.6 fusion.31
  92.2 0.3 fusion.10
  93.2 1.5 pad_maximum_fusion
  94.8 68.7 %reduce-scatter.5.cloned.1.call-done = f32[2,64,512]{2,1,0:T(8,128)} async-done(((f32[2,512,512]{2,1,0:T(8,128)}), f32[2,64,512]{2,1,0:T(8,128)}) %reduce-scatter.5.cloned.1.call-update) | async-done | bytes 262160 | tf_op jit(solution)/shard_map/reduce_scatter | solution.py:73
  163.4 50.3 %all-gather.2.cloned.1.call-done = f32[2,512,512]{2,1,0:T(8,128)} async-done(((f32[2,64,512]{2,1,0:T(8,128)}), f32[2,512,512]{2,1,0:T(8,128)}) %all-gather.2.cloned.1.call-update) | async-done | bytes 2097168 | tf_op jit(solution)/shard_map/all_gather | solution.py:76
  213.8 3.4 %add.92 = f32[2,512,512]{2,1,0:T(8,128)} add(f32[2,512,512]{2,1,0:T(8,128)S(1)} %copy-done, f32[2,512,512]{2,1,0:T(8,128)} %all-gather.2.cloned.1.call-done) | non-fusion elementwise | flops 524288 | bytes 6291456 | tf_op jit(solution)/shard_map/add | solution.py:77
  (48 shorter events, 2.7 us)
Async XLA Ops:
  7.2 59.9 %copy-start.1 = (bf16[2,16,2048]{2,1,0:T(8,128)(2,1)S(1)}, bf16[2,16,2048]{2,1,0:T(8,128)(2,1)}, u32[]{:S(2)}) copy-start(bf16[2,16,2048]{2,1,0:T(8,128)(2,1)} %param.5) | copy-start | bytes 393220
  9.6 9.6 %collective-permute-start = (bf16[2,16,2048]{2,1,0:T(8,128)(2,1)S(1)}, bf16[2,16,2048]{2,1,0:T(8,128)(2,1)S(1)}, u32[]{:S(2)}, u32[]{:S(2)}) collective-permute-start(bf16[2,16,2048]{2,1,0:T(8,128)(2,1)S(1)} %broadcast_select_fusion), channel_id=1, source_target_pairs={{0,4},{4,8},{8,12},{12,16},{16,20},{20,24},{24,28},{28,0},{1,5},{5... | collective-permute-start | bytes 393224 | tf_op jit(solution)/shard_map/ppermute | solution.py:53
  19.2 7.7 %collective-permute-start.1 = (bf16[2,16,2048]{2,1,0:T(8,128)(2,1)S(1)}, bf16[2,16,2048]{2,1,0:T(8,128)(2,1)S(1)}, u32[]{:S(2)}, u32[]{:S(2)}) collective-permute-start(bf16[2,16,2048]{2,1,0:T(8,128)(2,1)S(1)} %collective-permute-done), channel_id=1, source_target_pairs={{0,4},{4,8},{8,12},{12,16},{16,20},{20,24},{24,28},{28,0},{1,5},{5... | collective-permute-start | bytes 393224 | tf_op jit(solution)/shard_map/ppermute | solution.py:53
  26.8 7.7 %collective-permute-start.2 = (bf16[2,16,2048]{2,1,0:T(8,128)(2,1)S(1)}, bf16[2,16,2048]{2,1,0:T(8,128)(2,1)S(1)}, u32[]{:S(2)}, u32[]{:S(2)}) collective-permute-start(bf16[2,16,2048]{2,1,0:T(8,128)(2,1)S(1)} %collective-permute-done.1), channel_id=1, source_target_pairs={{0,4},{4,8},{8,12},{12,16},{16,20},{20,24},{24,28},{28,0},{1,5},{5... | collective-permute-start | bytes 393224 | tf_op jit(solution)/shard_map/ppermute | solution.py:53
  34.5 7.7 %collective-permute-start.3 = (bf16[2,16,2048]{2,1,0:T(8,128)(2,1)S(1)}, bf16[2,16,2048]{2,1,0:T(8,128)(2,1)S(1)}, u32[]{:S(2)}, u32[]{:S(2)}) collective-permute-start(bf16[2,16,2048]{2,1,0:T(8,128)(2,1)S(1)} %collective-permute-done.2), channel_id=1, source_target_pairs={{0,4},{4,8},{8,12},{12,16},{16,20},{20,24},{24,28},{28,0},{1,5},{5... | collective-permute-start | bytes 393224 | tf_op jit(solution)/shard_map/ppermute | solution.py:53
  42.1 8.9 %collective-permute-start.4 = (bf16[2,16,2048]{2,1,0:T(8,128)(2,1)S(1)}, bf16[2,16,2048]{2,1,0:T(8,128)(2,1)S(1)}, u32[]{:S(2)}, u32[]{:S(2)}) collective-permute-start(bf16[2,16,2048]{2,1,0:T(8,128)(2,1)S(1)} %collective-permute-done.3), channel_id=1, source_target_pairs={{0,4},{4,8},{8,12},{12,16},{16,20},{20,24},{24,28},{28,0},{1,5},{5... | collective-permute-start | bytes 393224 | tf_op jit(solution)/shard_map/ppermute | solution.py:53
  43.8 7.2 %all-to-all-start = ((bf16[4,2,2048]{2,1,0:T(2,128)(2,1)}), bf16[4,2,2048]{2,1,0:T(2,128)(2,1)S(1)}, u32[]{:S(2)}, u32[]{:S(2)}) async-start(bf16[4,2,2048]{2,1,0:T(2,128)(2,1)} %reshape.60), calls=%async_computation | async-start | bytes 65536 | tf_op jit(solution)/shard_map/all_to_all | solution.py:49
  47.0 43.2 %reduce-scatter.3.cloned.1.call-start = ((), (), s32[]{:S(2)}) async-start(), calls=%async_computation.3 | async-start | bytes 1310720 | tf_op jit(solution)/shard_map/reduce_scatter | solution.py:61
  51.1 8.2 %collective-permute-start.5 = (bf16[2,16,2048]{2,1,0:T(8,128)(2,1)S(1)}, bf16[2,16,2048]{2,1,0:T(8,128)(2,1)S(1)}, u32[]{:S(2)}, u32[]{:S(2)}) collective-permute-start(bf16[2,16,2048]{2,1,0:T(8,128)(2,1)S(1)} %collective-permute-done.4), channel_id=1, source_target_pairs={{0,4},{4,8},{8,12},{12,16},{16,20},{20,24},{24,28},{28,0},{1,5},{5... | collective-permute-start | bytes 393224 | tf_op jit(solution)/shard_map/ppermute | solution.py:53
  59.2 7.7 %collective-permute-start.6 = (bf16[2,16,2048]{2,1,0:T(8,128)(2,1)S(1)}, bf16[2,16,2048]{2,1,0:T(8,128)(2,1)S(1)}, u32[]{:S(2)}, u32[]{:S(2)}) collective-permute-start(bf16[2,16,2048]{2,1,0:T(8,128)(2,1)S(1)} %collective-permute-done.5), channel_id=1, source_target_pairs={{0,4},{4,8},{8,12},{12,16},{16,20},{20,24},{24,28},{28,0},{1,5},{5... | collective-permute-start | bytes 393224 | tf_op jit(solution)/shard_map/ppermute | solution.py:53
  69.4 94.0 %reduce-scatter.5.cloned.1.call-start = ((), (), s32[]{:S(2)}) async-start(), calls=%async_computation.4 | async-start | bytes 2359296 | tf_op jit(solution)/shard_map/reduce_scatter | solution.py:73
  94.7 119.1 %copy-start = (f32[2,512,512]{2,1,0:T(8,128)S(1)}, f32[2,512,512]{2,1,0:T(8,128)}, u32[]{:S(2)}) copy-start(f32[2,512,512]{2,1,0:T(8,128)} %param.7) | copy-start | bytes 6291460
  94.7 119.0 %all-gather.2.cloned.1.call-start = ((), (), s32[]{:S(2)}) async-start(), calls=%async_computation.5 | async-start | bytes 2359296 | tf_op jit(solution)/shard_map/all_gather | solution.py:76
Sparse Core Ops, SparseCore 0:
  69.6 20.6 reduce-scatter.2
  94.8 68.5 reduce-scatter.4
  165.6 48.0 all-gather.1
